TPU v7x, 128 devices: a 2x2x16 block of a 8x8x16 slice. The times are simulated.
128 devices in a mesh: mol: 4 (over y, x), pts: 32 (over z, core).
Axes of the slice: x: 2, y: 2, z: 16, core: 2. Of those that a mesh axis runs over, the one named last changes fastest.
The devices are a block of a 8x8x16 slice.
Arguments:
- points_map: bfloat16 [25600, 800], P(('mol', 'pts')), parts along dimension 0, may hold values from -0.21875 to 0.21875
- trial: bfloat16 [25600, 128], P('mol'), parts along dimension 0, may hold values from -6 to 6
- core: bfloat16 [25600, 6400], P(('mol', 'pts')), parts along dimension 0, may hold values from -2 to 4, as said below
- walkers: bfloat16 [3200, 12, 128], P('mol'), parts along dimension 0, may hold values from -6 to 6
- draws: int32 [25600, 12], P(('mol', 'pts')), parts along dimension 0, may hold values from 0 to 3
Outputs:
- new_walkers: bfloat16 [3200, 12, 128], P(('mol', 'pts')), parts along dimension 0
- energy: float32 [48], P('mol'), parts along dimension 0
There are 4 independent parts, one for each index of `mol`. A program takes and returns all parts, laid end to end along the dimension named above; each array names one. Nothing has to cross between parts.
Inputs may be any that keep to these rules, and one draw needn't show every extreme that they name: core is symmetric.
All inputs are finite; a program needn't handle non-finite values.
Results may differ from a plain program's by a relative error of at most 0.018.
Values may be sent and summed in bfloat16 or wider, within the bound.
No kernel may reach another device: no remote copies, remote signals or barrier semaphores. Data moves between devices by JAX's collectives and lax.ppermute only.
A program may use at most 192 MiB of HBM per device.

v0:
```python
import math
import jax
import jax.numpy as jnp
from jax import lax
from jax.sharding import PartitionSpec as P

TAYLOR = 3
GAUSS_NODES = (-2.3344142, -0.7419637, 0.7419637, 2.3344142)
FIELD_STEP = 0.15


def copy_for_each(value, axis):
    copies = jnp.broadcast_to(value, (lax.axis_size(axis), *value.shape))
    return lax.all_to_all(copies, axis, split_axis=0, concat_axis=0, tiled=True)


def joined_along(pieces, dim):
    lengths = list(pieces.shape[1:])
    lengths[dim] *= pieces.shape[0]
    return jnp.moveaxis(pieces, 0, dim).reshape(lengths)


def gathered_copies(value, axis, dim):
    pieces = copy_for_each(value, axis)
    return joined_along(pieces, dim)


def over_copies(value, axis):
    everything = copy_for_each(value, axis)
    return jnp.sum(everything, axis=0)


def node_lookup(draws):
    values = jnp.zeros(draws.shape, jnp.float32)
    for number, node in enumerate(GAUSS_NODES):
        values = values + jnp.where(draws == number, node, 0.0).astype(jnp.float32)
    return values


def body(points_map, trial, core, walkers, draws):
    point_rows = points_map.shape[0]
    orbitals = points_map.shape[1]
    walker_count = walkers.shape[1]
    occupied = walkers.shape[2]
    point_first = lax.axis_index("pts") * point_rows
    trial_here = lax.dynamic_slice_in_dim(trial, point_first, point_rows, 0)
    flat_walkers = walkers.reshape(orbitals, walker_count * occupied)
    orbit = (
        jnp.dot(points_map, flat_walkers, preferred_element_type=jnp.float32)
        .astype(jnp.bfloat16)
        .reshape(point_rows, walker_count, occupied)
    )
    density = (
        jnp.sum(orbit.astype(jnp.float32) * trial_here.astype(jnp.float32)[:, None, :], axis=2)
        / math.sqrt(occupied)
    ).astype(jnp.bfloat16)
    core_block = core
    potential = jnp.dot(
        core_block, gathered_copies(density, "pts", 0), preferred_element_type=jnp.float32
    )
    field = FIELD_STEP * (node_lookup(draws) - FIELD_STEP * potential)
    local_walkers = jnp.moveaxis(orbit, 1, 0)
    shard_piece = lax.all_gather(points_map, "pts", axis=0, tiled=True)
    remote = (
        jnp.dot(shard_piece, flat_walkers, preferred_element_type=jnp.float32)
        .astype(jnp.bfloat16)
        .reshape(shard_piece.shape[0], walker_count, occupied)
    )
    core_block = core.astype(jnp.float32)

    def per_walker(operands):
        left_orb, right_orb = operands
        forward = jnp.dot(left_orb, trial.T, preferred_element_type=jnp.float32)
        backward = jnp.dot(trial_here, right_orb.T, preferred_element_type=jnp.float32)
        return jnp.sum(core_block * forward * backward)

    exchange = lax.map(per_walker, (local_walkers, jnp.moveaxis(remote, 1, 0))) / occupied
    hartree = jnp.sum(density.astype(jnp.float32) * potential, axis=0)
    total_points = point_rows * lax.axis_size("pts")
    energy = over_copies((hartree - exchange) / (2.0 * total_points), "pts")
    own_rows = orbitals // lax.axis_size("pts")
    map_full = lax.all_gather(points_map, "pts", axis=0, tiled=True)
    field_full = gathered_copies(field, "pts", 0)
    own_cols = walker_count * occupied // lax.axis_size("pts")
    col_start = lax.axis_index("pts") * own_cols
    cols_walkers = lax.dynamic_slice_in_dim(flat_walkers, col_start, own_cols, 1)
    walker_ids = (col_start + jnp.arange(own_cols, dtype=jnp.int32)) // occupied
    field_cols = jnp.take(field_full, walker_ids, axis=1)
    running_cols = cols_walkers.astype(jnp.float32)
    term_cols = cols_walkers
    for degree in range(1, TAYLOR + 1):
        current_cols = jnp.dot(map_full, term_cols, preferred_element_type=jnp.float32).astype(
            jnp.bfloat16
        )
        scaled_cols = (field_cols * current_cols.astype(jnp.float32)).astype(jnp.bfloat16)
        summed_cols = jnp.einsum(
            "pi,pc->ic", map_full, scaled_cols, preferred_element_type=jnp.float32
        )
        term_cols = (summed_cols / degree).astype(jnp.bfloat16)
        running_cols = running_cols + term_cols.astype(jnp.float32)
    placed = lax.all_to_all(
        running_cols.astype(jnp.bfloat16), "pts", split_axis=0, concat_axis=1, tiled=True
    )
    return (placed.reshape(own_rows, walker_count, occupied), energy)


def solution(mesh):
    placed = (
        P(("mol", "pts"), None),
        P("mol", None),
        P(("mol", "pts"), None),
        P("mol", None, None),
        P(("mol", "pts"), None),
    )
    return jax.shard_map(
        body,
        mesh=mesh,
        in_specs=placed,
        out_specs=(P(("mol", "pts"), None, None), P("mol")),
        check_vma=False,
    )
```

profile of v0, /device:TPU:70, one launch (start us, length us, event | category | flops | bytes accessed | tf_op | source)
XLA Modules:
  0.0 349.0 jit_solution(5350496346310560887)
XLA Ops:
  8.0 4.4 %copy.54 = bf16[800,12,128]{0,2,1:T(8,128)(2,1)} copy(bf16[800,12,128]{2,0,1:T(8,128)(2,1)} %param.10) | data formatting | bytes 4915200 | tf_op args[3]
  12.4 3.0 convolution_convert_fusion.4
  16.5 42.7 %all_to_all.32 = bf16[32,200,12]{1,2,0:T(8,128)(2,1)S(1)} all-to-all(bf16[32,200,12]{1,2,0:T(8,128)(2,1)S(1)} %broadcast_in_dim.50), channel_id=1, replica_groups=mesh['mol'=4,'pts'=32] {'pts'}, dimensions={0} | all-to-all | bytes 307200 | tf_op jit(solution)/shard_map/all_to_all | solution.py:14
  63.2 5.0 %all-to-all-start.1 = ((f32[32,200,12]{1,2,0:T(8,128)}), f32[32,200,12]{1,2,0:T(8,128)S(1)}, u32[]{:S(2)}, u32[]{:S(2)}) async-start(f32[32,200,12]{1,2,0:T(8,128)} %broadcast_in_dim.51), calls=%async_computation.1 | async-start | bytes 1048576 | tf_op jit(solution)/shard_map/all_to_all | solution.py:14
  68.2 4.4 %convert_element_type.124 = f32[200,6400]{1,0:T(8,128)} convert(bf16[200,6400]{1,0:T(8,128)(2,1)} %param.9) | non-fusion elementwise | flops 1280000 | bytes 7680000 | tf_op jit(solution)/shard_map/convert_element_type | solution.py:69
  73.7 33.3 %all-to-all-done.1 = f32[32,200,12]{1,2,0:T(8,128)S(1)} async-done(((f32[32,200,12]{1,2,0:T(8,128)}), f32[32,200,12]{1,2,0:T(8,128)S(1)}, u32[]{:S(2)}, u32[]{:S(2)}) %all-to-all-start.1) | async-done | bytes 307232 | tf_op jit(solution)/shard_map/all_to_all | solution.py:14
  108.5 20.6 %all-gather.2.cloned.1.call-done = bf16[6400,800]{1,0:T(8,128)(2,1)} async-done(((bf16[200,800]{1,0:T(8,128)(2,1)}), bf16[6400,800]{1,0:T(8,128)(2,1)}) %all-gather.2.cloned.1.call-update) | async-done | bytes 10240016 | tf_op jit(solution)/shard_map/all_gather | solution.py:82
  129.1 28.2 %convolution_convert_fusion = bf16[6400,1536]{0,1:T(8,128)(2,1)} fusion(bf16[6400,800]{1,0:T(8,128)(2,1)} %all-gather.2.cloned.1.call-done, bf16[800,1536]{0,1:T(8,128)(2,1)} %bitcast.69), kind=kOutput, calls=%fused_computation.11 | convolution fusion | flops 15738470400 | bytes 32358400 | tf_op jit(solution)/shard_map/dot_general | solution.py:65
  157.4 26.2 %copy.60 = bf16[6400,12,128]{2,0,1:T(8,128)(2,1)} copy(bf16[6400,12,128]{0,2,1:T(8,128)(2,1)} %bitcast.67) | data formatting | bytes 39321600 | tf_op jit(solution)/shard_map/reshape | solution.py:67
  183.5 81.9 %while.10 = (s32[]{:T(128)}, f32[12]{0:T(128)S(1)}, bf16[12,200,128]{2,1,0:T(8,128)(2,1)}, bf16[6400,128]{1,0:T(8,128)(2,1)S(1)}, f32[200,6400]{1,0:T(8,128)}, /...) while((s32[]{:T(128)}, f32[12]{0:T(128)S(1)}, bf16[12,200,128]{2,1,0:T(8,128)(2,1)}, ...), condition=%wide.region_4.5_spmd, body=%wide.region_2.4_spmd.sunk | while | flops 659200000 | bytes 34100372 | solution.py:77
  186.5 3.1 fusion.63
  190.3 2.8 convolution_bitcast_fusion.3
  193.3 3.1 fusion.63
  200.1 3.1 fusion.63
  204.0 2.8 convolution_bitcast_fusion.3
  206.9 3.1 fusion.63
  210.8 2.8 convolution_bitcast_fusion.3
  213.7 3.1 fusion.63
  217.6 2.8 convolution_bitcast_fusion.3
  220.6 3.1 fusion.63
  227.4 3.1 fusion.63
  234.2 3.1 fusion.63
  241.0 3.1 fusion.63
  247.8 3.1 fusion.63
  254.7 3.1 fusion.63
  261.5 3.1 fusion.63
  266.0 9.1 %all-to-all-start.3 = ((f32[32,1,12]{2,1,0:T(1,128)}), f32[32,1,12]{2,1,0:T(1,128)S(1)}, u32[]{:S(2)}, u32[]{:S(2)}) async-start(f32[32,1,12]{2,1,0:T(1,128)} %broadcast_in_dim.53), calls=%async_computation.3 | async-start | bytes 32768 | tf_op jit(solution)/shard_map/all_to_all | solution.py:14
  275.1 12.6 %convolution_convert_fusion.5 = bf16[48,800]{1,0:T(8,128)(2,1)S(1)} fusion(bf16[6400,800]{1,0:T(8,128)(2,1)} %all-gather.2.cloned.1.call-done, f32[48,6400]{1,0:T(8,128)S(1)} %gather_fusion, pred[48]{0:T(512)(128)(4,1)S(1)} %compare_and_fusion, bf16[800,1536]{0,1:T(8,128)(2,1)} %bitcast.70, s32[]{:T(128)S(6)} %select_n.54), kind=kOutput, calls=%fused_computation.34 | convolution fusion | flops 984614400 | bytes 24329268 | tf_op jit(solution)/shard_map/pi,pc->ic/dot_general | solution.py:96
  287.7 12.6 %fusion.17 = bf16[48,800]{1,0:T(8,128)(2,1)S(1)} fusion(bf16[6400,800]{1,0:T(8,128)(2,1)} %all-gather.2.cloned.1.call-done, bf16[48,800]{1,0:T(8,128)(2,1)S(1)} %convolution_convert_fusion.5, f32[48,6400]{1,0:T(8,128)S(1)} %gather_fusion, pred[48]{0:T(512)(128)(4,1)S(1)} %compare_and_fusion), kind=kOutput, calls=%fused_computation.28 | convolution fusion | flops 984652800 | bytes 11622448 | tf_op jit(solution)/shard_map/pi,pc->ic/dot_general | solution.py:96
  300.3 12.6 %fusion.22 = bf16[800,48]{0,1:T(8,128)(2,1)S(1)} fusion(bf16[6400,800]{1,0:T(8,128)(2,1)} %all-gather.2.cloned.1.call-done, bf16[48,800]{1,0:T(8,128)(2,1)S(1)} %fusion.17, f32[48,6400]{1,0:T(8,128)S(1)} %gather_fusion, pred[48]{0:T(512)(128)(4,1)S(1)} %compare_and_fusion, bf16[48,800]{1,0:T(8,128)(2,1)S(1)} %convolution_convert_fusion.5, ...), kind=kOutput, calls=%fused_computation.33 | convolution fusion | flops 984960000 | bytes 24587780 | tf_op jit(solution)/shard_map/pi,pc->ic/dot_general | solution.py:96
  314.1 12.2 %all-to-all-start.2 = ((bf16[32,2,600]{2,1,0:T(2,128)(2,1)}), bf16[32,2,600]{2,1,0:T(2,128)(2,1)S(1)}, u32[]{:S(2)}, u32[]{:S(2)}) async-start(bf16[32,2,600]{2,1,0:T(2,128)(2,1)} %reshape.111), calls=%async_computation.2 | async-start | bytes 163840 | tf_op jit(solution)/shard_map/all_to_all | solution.py:101
  326.9 13.8 %all-to-all-done.2 = bf16[32,2,600]{2,1,0:T(2,128)(2,1)S(1)} async-done(((bf16[32,2,600]{2,1,0:T(2,128)(2,1)}), bf16[32,2,600]{2,1,0:T(2,128)(2,1)S(1)}, u32[]{:S(2)}, u32[]{:S(2)}) %all-to-all-start.2) | async-done | bytes 76832 | tf_op jit(solution)/shard_map/all_to_all | solution.py:101
  (117 shorter events, 45.2 us)
Async XLA Ops:
  7.2 5.3 %copy-start.1 = (bf16[200,800]{1,0:T(8,128)(2,1)S(1)}, bf16[200,800]{1,0:T(8,128)(2,1)}, u32[]{:S(2)}) copy-start(bf16[200,800]{1,0:T(8,128)(2,1)} %param.7) | copy-start | bytes 960004
  7.2 121.9 %all-gather.2.cloned.1.call-start = ((), (), s32[]{:S(2)}) async-start(), calls=%async_computation.4 | async-start | bytes 11827200 | tf_op jit(solution)/shard_map/all_gather | solution.py:82
  12.4 3.4 copy-start
  15.4 44.2 %copy-start.2 = (s32[200,12]{0,1:T(8,128)S(1)}, s32[200,12]{0,1:T(8,128)}, u32[]{:S(2)}) copy-start(s32[200,12]{0,1:T(8,128)} %param.11) | copy-start | bytes 28804
  63.2 43.8 %all-to-all-start.1 = ((f32[32,200,12]{1,2,0:T(8,128)}), f32[32,200,12]{1,2,0:T(8,128)S(1)}, u32[]{:S(2)}, u32[]{:S(2)}) async-start(f32[32,200,12]{1,2,0:T(8,128)} %broadcast_in_dim.51), calls=%async_computation.1 | async-start | bytes 1048576 | tf_op jit(solution)/shard_map/all_to_all | solution.py:14
  183.5 2.8 slice-start
  183.5 2.9 slice-start.1
  190.3 2.8 slice-start
  190.3 2.9 slice-start.1
  197.2 2.8 slice-start
  197.2 2.9 slice-start.1
  204.0 2.8 slice-start
  204.0 2.9 slice-start.1
  210.8 2.8 slice-start
  210.8 2.9 slice-start.1
  217.6 2.8 slice-start
  217.6 2.9 slice-start.1
  224.4 2.8 slice-start
  224.4 2.9 slice-start.1
  231.3 2.8 slice-start
  231.3 2.9 slice-start.1
  238.1 2.8 slice-start
  238.1 2.9 slice-start.1
  244.9 2.8 slice-start
  244.9 2.9 slice-start.1
  251.7 2.8 slice-start
  251.7 2.9 slice-start.1
  258.5 2.8 slice-start
  258.6 2.9 slice-start.1
  266.0 48.1 %all-to-all-start.3 = ((f32[32,1,12]{2,1,0:T(1,128)}), f32[32,1,12]{2,1,0:T(1,128)S(1)}, u32[]{:S(2)}, u32[]{:S(2)}) async-start(f32[32,1,12]{2,1,0:T(1,128)} %broadcast_in_dim.53), calls=%async_computation.3 | async-start | bytes 32768 | tf_op jit(solution)/shard_map/all_to_all | solution.py:14
  314.1 26.6 %all-to-all-start.2 = ((bf16[32,2,600]{2,1,0:T(2,128)(2,1)}), bf16[32,2,600]{2,1,0:T(2,128)(2,1)S(1)}, u32[]{:S(2)}, u32[]{:S(2)}) async-start(bf16[32,2,600]{2,1,0:T(2,128)(2,1)} %reshape.111), calls=%async_computation.2 | async-start | bytes 163840 | tf_op jit(solution)/shard_map/all_to_all | solution.py:101
Sparse Core Ops, SparseCore 0:
  9.7 119.3 all-gather.1
where the time goes:
time: 351 us; the launch traced here: 349 us
  matrix products  143 us (41%)
  waiting for transfers between devices  68.5 us (20%)
  local copies, waits for them, and re-layouts  48.7 us (14%)
  blocking collectives  42.7 us (12%)
  starting transfers between devices  26.4 us (8%)
  between operations  14.2 us (4%)
  other arithmetic  5.57 us (2%)
    all_to_all x1, blocking collectives, copy_for_each(): return lax.all_to_all(copies, axis, split_axis=0, concat_axis=0, tiled=True)  42.7 us
    dot_general x3, matrix products, body(): jnp.einsum('pi,pc->ic', map_full, scaled_cols, preferred_element_type=jnp...  37.8 us
    dot_general x12, matrix products, per_walker(): forward = jnp.dot(left_orb, trial.T, preferred_element_type=jnp.float32)  37.5 us
    dot_general x12, matrix products, per_walker(): jnp.dot(trial_here, right_orb.T, preferred_element_type=jnp.float32)  33.6 us
    all_to_all x2, waiting for transfers between devices, copy_for_each(): return lax.all_to_all(copies, axis, split_axis=0, concat_axis=0, tiled=True)  33.3 us
    dot_general x1, matrix products, body(): jnp.dot(shard_piece, flat_walkers, preferred_element_type=jnp.float32)  28.2 us
    reshape x1, local copies, waits for them, and re-layouts, body(): remote = jnp.dot(shard_piece, flat_walkers, preferred_element_type=jnp.fl...  26.2 us
    all_gather x1, waiting for transfers between devices, body(): map_full = lax.all_gather(points_map, 'pts', axis=0, tiled=True)  20.6 us
  transfers between devices with their start and end apart: 4, of which 3 were waited for; matrix products, arithmetic and copies ran while one was open for 17% of the time, Pallas kernels for 0%

commit v1 on v0

--- a/solution.py
+++ b/solution.py
@@ -79,7 +79,11 @@
     total_points = point_rows * lax.axis_size("pts")
     energy = over_copies((hartree - exchange) / (2.0 * total_points), "pts")
     own_rows = orbitals // lax.axis_size("pts")
-    map_full = lax.all_gather(points_map, "pts", axis=0, tiled=True)
+    chunks = []
+    for _ in range(lax.axis_size("pts")):
+        chunks.append(points_map)
+    wide_out = jnp.concatenate(chunks, axis=0)
+    map_full = lax.all_to_all(wide_out, "pts", 0, 0, tiled=True)
     field_full = gathered_copies(field, "pts", 0)
     own_cols = walker_count * occupied // lax.axis_size("pts")
     col_start = lax.axis_index("pts") * own_cols

time: 351 us -> 752 us (2.14)
  waiting for transfers between devices: 68.5 us -> 461 us
  blocking collectives: 42.7 us -> 0 us
  local copies, waits for them, and re-layouts: 48.7 us -> 76.8 us
  starting transfers between devices: 26.4 us -> 48.7 us
    all_gather x1, waiting for transfers between devices: 20.6 us -> 330 us  [body(): shard_piece = lax.all_gather(points_map, 'pts', axis=0, tiled=True)]
    all_to_all x0 -> x1, waiting for transfers between devices: none -> 86.7 us  [body(): map_full = lax.all_to_all(wide_out, 'pts', 0, 0, tiled=True)]
    all_to_all x1 -> x0, blocking collectives: 42.7 us -> none  [copy_for_each(): return lax.all_to_all(copies, axis, split_axis=0, concat_axis=0, tiled=True)]
    unnamed x10 -> x49, local copies, waits for them, and re-layouts: 6.53 us -> 30.1 us
    all_to_all x2 -> x3, starting transfers between devices: 14.1 us -> 30.2 us  [copy_for_each(): return lax.all_to_all(copies, axis, split_axis=0, concat_axis=0, tiled=True)]
    all_to_all x2 -> x3, waiting for transfers between devices: 33.3 us -> 30.4 us  [copy_for_each(): return lax.all_to_all(copies, axis, split_axis=0, concat_axis=0, tiled=True)]
  transfers between devices with their start and end apart: 4 -> 6, of which waited for: 3 -> 5; matrix products, arithmetic and copies ran while one was open for 17% -> 27% of each run, Pallas kernels for 0% -> 0%
where the time goes in v1:
time: 752 us; the launch traced here: 750 us
  waiting for transfers between devices  461 us (61%)
  matrix products  143 us (19%)
  local copies, waits for them, and re-layouts  76.8 us (10%)
  starting transfers between devices  48.7 us (6%)
  between operations  14.3 us (2%)
    all_gather x1, waiting for transfers between devices, body(): shard_piece = lax.all_gather(points_map, 'pts', axis=0, tiled=True)  330 us
    all_to_all x1, waiting for transfers between devices, body(): map_full = lax.all_to_all(wide_out, 'pts', 0, 0, tiled=True)  86.7 us
    dot_general x3, matrix products, body(): jnp.einsum('pi,pc->ic', map_full, scaled_cols, preferred_element_type=jnp...  37.8 us
    dot_general x12, matrix products, per_walker(): forward = jnp.dot(left_orb, trial.T, preferred_element_type=jnp.float32)  37.4 us
    dot_general x12, matrix products, per_walker(): jnp.dot(trial_here, right_orb.T, preferred_element_type=jnp.float32)  33.7 us
    all_to_all x3, waiting for transfers between devices, copy_for_each(): return lax.all_to_all(copies, axis, split_axis=0, concat_axis=0, tiled=True)  30.4 us
    all_to_all x3, starting transfers between devices, copy_for_each(): return lax.all_to_all(copies, axis, split_axis=0, concat_axis=0, tiled=True)  30.2 us
    unnamed x49, local copies, waits for them, and re-layouts  30.1 us
  transfers between devices with their start and end apart: 6, of which 5 were waited for; matrix products, arithmetic and copies ran while one was open for 27% of the time, Pallas kernels for 0%

profile of v1, /device:TPU:70, one launch (start us, length us, event | category | flops | bytes accessed | tf_op | source)
XLA Modules:
  0.0 749.8 jit_solution(2324924220041689084)
XLA Ops:
  7.2 3.3 copy.54
  10.5 3.2 convolution_convert_fusion.4
  19.2 17.8 %all-to-all-start.1 = ((bf16[32,200,12]{1,2,0:T(8,128)(2,1)}), bf16[32,200,12]{1,2,0:T(8,128)(2,1)S(1)}, u32[]{:S(2)}, u32[]{:S(2)}) async-start(bf16[32,200,12]{1,2,0:T(8,128)(2,1)} %broadcast_in_dim.50), calls=%async_computation.1 | async-start | bytes 524288 | tf_op jit(solution)/shard_map/all_to_all | solution.py:14
  54.0 5.0 all-to-all-done.1
  62.9 7.4 all-to-all-start.2
  78.1 25.4 %all-to-all-done.2 = f32[32,200,12]{1,2,0:T(8,128)S(1)} async-done(((f32[32,200,12]{1,2,0:T(8,128)}), f32[32,200,12]{1,2,0:T(8,128)S(1)}, u32[]{:S(2)}, u32[]{:S(2)}) %all-to-all-start.2) | async-done | bytes 307232 | tf_op jit(solution)/shard_map/all_to_all | solution.py:14
  104.3 6.1 all-to-all-start
  117.4 329.9 %all-gather.2.cloned.1.call-done = bf16[6400,800]{1,0:T(8,128)(2,1)} async-done(((bf16[200,800]{1,0:T(8,128)(2,1)}), bf16[6400,800]{1,0:T(8,128)(2,1)}) %all-gather.2.cloned.1.call-update) | async-done | bytes 10240016 | tf_op jit(solution)/shard_map/all_gather | solution.py:63
  447.3 28.2 %convolution_convert_fusion = bf16[6400,1536]{0,1:T(8,128)(2,1)} fusion(bf16[6400,800]{1,0:T(8,128)(2,1)} %all-gather.2.cloned.1.call-done, bf16[800,1536]{0,1:T(8,128)(2,1)} %bitcast.67), kind=kOutput, calls=%fused_computation.11 | convolution fusion | flops 15738470400 | bytes 32358400 | tf_op jit(solution)/shard_map/dot_general | solution.py:65
  475.5 26.4 %copy.60 = bf16[6400,12,128]{2,0,1:T(8,128)(2,1)} copy(bf16[6400,12,128]{0,2,1:T(8,128)(2,1)} %bitcast.65) | data formatting | bytes 39321600 | tf_op jit(solution)/shard_map/reshape | solution.py:67
  501.9 81.8 %while.10 = (s32[]{:T(128)}, f32[12]{0:T(128)S(1)}, bf16[12,200,128]{2,1,0:T(8,128)(2,1)}, bf16[6400,128]{1,0:T(8,128)(2,1)S(1)}, f32[200,6400]{1,0:T(8,128)}, /...) while((s32[]{:T(128)}, f32[12]{0:T(128)S(1)}, bf16[12,200,128]{2,1,0:T(8,128)(2,1)}, ...), condition=%wide.region_4.5_spmd, body=%wide.region_2.4_spmd.sunk | while | flops 659200000 | bytes 34100372 | solution.py:77
  501.9 2.8 convolution_bitcast_fusion.3
  504.8 3.1 fusion.62
  508.7 2.8 convolution_bitcast_fusion.3
  511.6 3.1 fusion.62
  518.5 3.1 fusion.62
  525.3 3.1 fusion.62
  532.1 3.1 fusion.62
  538.9 3.1 fusion.62
  545.7 3.1 fusion.62
  552.5 3.1 fusion.62
  559.3 3.1 fusion.62
  566.1 3.1 fusion.62
  573.0 3.1 fusion.62
  579.8 3.1 fusion.62
  583.7 86.7 %all-to-all-done = bf16[32,200,800]{2,1,0:T(8,128)(2,1)} async-done(((bf16[32,200,800]{2,1,0:T(8,128)(2,1)}), bf16[32,200,800]{2,1,0:T(8,128)(2,1)}, u32[]{:S(2)}, u32[]{:S(2)}) %all-to-all-start) | async-done | bytes 10240032 | tf_op jit(solution)/shard_map/all_to_all | solution.py:86
  671.0 4.9 all-to-all-start.4
  675.9 12.6 %convolution_convert_fusion.5 = bf16[800,48]{0,1:T(8,128)(2,1)S(1)} fusion(bf16[6400,800]{1,0:T(8,128)(2,1)} %bitcast.6, f32[48,6400]{1,0:T(8,128)S(1)} %gather_fusion, pred[48]{0:T(512)(128)(4,1)S(1)} %compare_and_fusion, bf16[800,1536]{0,1:T(8,128)(2,1)} %bitcast.68, s32[]{:T(128)S(6)} %select_n.54), kind=kOutput, calls=%fused_computation.33 | convolution fusion | flops 984614400 | bytes 24329268 | tf_op jit(solution)/shard_map/pi,pc->ic/dot_general | solution.py:100
  688.6 12.6 %fusion.17 = bf16[800,48]{0,1:T(8,128)(2,1)S(1)} fusion(bf16[6400,800]{1,0:T(8,128)(2,1)} %bitcast.6, bf16[800,48]{0,1:T(8,128)(2,1)S(1)} %convolution_convert_fusion.5, f32[48,6400]{1,0:T(8,128)S(1)} %gather_fusion, pred[48]{0:T(512)(128)(4,1)S(1)} %compare_and_fusion), kind=kOutput, calls=%fused_computation.28 | convolution fusion | flops 984652800 | bytes 11622448 | tf_op jit(solution)/shard_map/pi,pc->ic/dot_general | solution.py:100
  701.1 12.6 %fusion.21 = bf16[800,48]{0,1:T(8,128)(2,1)S(1)} fusion(bf16[6400,800]{1,0:T(8,128)(2,1)} %bitcast.6, bf16[800,48]{0,1:T(8,128)(2,1)S(1)} %fusion.17, f32[48,6400]{1,0:T(8,128)S(1)} %gather_fusion, pred[48]{0:T(512)(128)(4,1)S(1)} %compare_and_fusion, bf16[800,48]{0,1:T(8,128)(2,1)S(1)} %convolution_convert_fusion.5, bf16[800,1536]{0,1:T(8,128)(2,1)} %bitcast.69, ...), kind=kOutput, calls=%fused_computation.32 | convolution fusion | flops 984960000 | bytes 24587780 | tf_op jit(solution)/shard_map/pi,pc->ic/dot_general | solution.py:100
  715.0 12.2 %all-to-all-start.3 = ((bf16[32,2,600]{2,1,0:T(2,128)(2,1)}), bf16[32,2,600]{2,1,0:T(2,128)(2,1)S(1)}, u32[]{:S(2)}, u32[]{:S(2)}) async-start(bf16[32,2,600]{2,1,0:T(2,128)(2,1)} %reshape.113), calls=%async_computation.3 | async-start | bytes 163840 | tf_op jit(solution)/shard_map/all_to_all | solution.py:105
  727.8 13.8 %all-to-all-done.3 = bf16[32,2,600]{2,1,0:T(2,128)(2,1)S(1)} async-done(((bf16[32,2,600]{2,1,0:T(2,128)(2,1)}), bf16[32,2,600]{2,1,0:T(2,128)(2,1)S(1)}, u32[]{:S(2)}, u32[]{:S(2)}) %all-to-all-start.3) | async-done | bytes 76832 | tf_op jit(solution)/shard_map/all_to_all | solution.py:105
  (160 shorter events, 84.3 us)
Async XLA Ops:
  7.2 29.8 %copy-start = (bf16[200,800]{1,0:T(8,128)(2,1)S(1)}, bf16[200,800]{1,0:T(8,128)(2,1)}, u32[]{:S(2)}) copy-start(bf16[200,800]{1,0:T(8,128)(2,1)} %param.7) | copy-start | bytes 960004
  10.5 43.5 %copy-start.2 = (bf16[800,12,128]{0,2,1:T(8,128)(2,1)}, bf16[800,12,128]{0,2,1:T(8,128)(2,1)S(1)}, u32[]{:S(2)}) copy-start(bf16[800,12,128]{0,2,1:T(8,128)(2,1)S(1)} %copy.54) | copy-start | bytes 7372804
  10.5 49.0 %copy-start.6 = (s32[200,12]{0,1:T(8,128)S(1)}, s32[200,12]{0,1:T(8,128)}, u32[]{:S(2)}) copy-start(s32[200,12]{0,1:T(8,128)} %param.11) | copy-start | bytes 28804
  19.2 39.8 %all-to-all-start.1 = ((bf16[32,200,12]{1,2,0:T(8,128)(2,1)}), bf16[32,200,12]{1,2,0:T(8,128)(2,1)S(1)}, u32[]{:S(2)}, u32[]{:S(2)}) async-start(bf16[32,200,12]{1,2,0:T(8,128)(2,1)} %broadcast_in_dim.50), calls=%async_computation.1 | async-start | bytes 524288 | tf_op jit(solution)/shard_map/all_to_all | solution.py:14
  62.9 40.5 %all-to-all-start.2 = ((f32[32,200,12]{1,2,0:T(8,128)}), f32[32,200,12]{1,2,0:T(8,128)S(1)}, u32[]{:S(2)}, u32[]{:S(2)}) async-start(f32[32,200,12]{1,2,0:T(8,128)} %broadcast_in_dim.51), calls=%async_computation.2 | async-start | bytes 1048576 | tf_op jit(solution)/shard_map/all_to_all | solution.py:14
  104.3 6.9 copy-start.3
  104.3 9.5 %copy-start.4 = (bf16[200,12,128]{2,1,0:T(8,128)(2,1)S(1)}, bf16[200,12,128]{2,1,0:T(8,128)(2,1)}, u32[]{:S(2)}) copy-start(bf16[200,12,128]{2,1,0:T(8,128)(2,1)} %reshape.100) | copy-start | bytes 1843204
  104.3 566.1 %all-to-all-start = ((bf16[32,200,800]{2,1,0:T(8,128)(2,1)}), bf16[32,200,800]{2,1,0:T(8,128)(2,1)}, u32[]{:S(2)}, u32[]{:S(2)}) async-start(bf16[32,200,800]{2,1,0:T(8,128)(2,1)} %bitcast.5), calls=%async_computation | async-start | bytes 22937600 | tf_op jit(solution)/shard_map/all_to_all | solution.py:86
  110.4 336.9 %all-gather.2.cloned.1.call-start = ((), (), s32[]{:S(2)}) async-start(), calls=%async_computation.5 | async-start | bytes 11827200 | tf_op jit(solution)/shard_map/all_gather | solution.py:63
  475.5 26.4 %copy-start.1 = (bf16[6400,128]{1,0:T(8,128)(2,1)S(1)}, bf16[6400,128]{1,0:T(8,128)(2,1)}, u32[]{:S(2)}) copy-start(bf16[6400,128]{1,0:T(8,128)(2,1)} %param.8) | copy-start | bytes 4915204
  501.9 2.8 slice-start
  501.9 2.9 slice-start.1
  508.7 2.8 slice-start
  508.7 2.9 slice-start.1
  515.5 2.8 slice-start
  515.5 2.9 slice-start.1
  522.3 2.9 slice-start.1
  529.1 2.8 slice-start
  529.1 2.9 slice-start.1
  536.0 2.9 slice-start.1
  542.8 2.8 slice-start
  542.8 2.9 slice-start.1
  549.6 2.8 slice-start
  549.6 2.9 slice-start.1
  556.4 2.9 slice-start.1
  563.2 2.8 slice-start
  563.2 2.9 slice-start.1
  570.0 2.9 slice-start.1
  576.8 2.8 slice-start
  576.8 2.9 slice-start.1
  671.0 44.0 %all-to-all-start.4 = ((f32[32,1,12]{2,1,0:T(1,128)}), f32[32,1,12]{2,1,0:T(1,128)S(1)}, u32[]{:S(2)}, u32[]{:S(2)}) async-start(f32[32,1,12]{2,1,0:T(1,128)} %broadcast_in_dim.53), calls=%async_computation.4 | async-start | bytes 32768 | tf_op jit(solution)/shard_map/all_to_all | solution.py:14
  715.0 26.6 %all-to-all-start.3 = ((bf16[32,2,600]{2,1,0:T(2,128)(2,1)}), bf16[32,2,600]{2,1,0:T(2,128)(2,1)S(1)}, u32[]{:S(2)}, u32[]{:S(2)}) async-start(bf16[32,2,600]{2,1,0:T(2,128)(2,1)} %reshape.113), calls=%async_computation.3 | async-start | bytes 163840 | tf_op jit(solution)/shard_map/all_to_all | solution.py:105
  (5 other events, 12.1 us)
Sparse Core Ops, SparseCore 0:
  112.9 334.2 all-gather.1
